TPU v7x, 256 devices: a whole 4x4x8 slice. The times are simulated.
256 devices in a mesh: expert: 8 (over x, core), shard: 32 (over z, y).
Axes of the slice: x: 4, y: 4, z: 8, core: 2. Of those that a mesh axis runs over, the one named last changes fastest.
Arguments:
- w_gate: float32 [64, 2048, 1408], P('expert', 'shard'), may hold values from -0.25 to 0.25
- w_up: float32 [64, 2048, 1408], P('expert', 'shard'), may hold values from -0.25 to 0.25
- router_weight: float32 [2048, 64], P('shard', 'expert'), may hold values from -0.125 to 0.125
- router_gain: float32 [2048], P('shard'), may hold values from 0.25 to 1.75
Outputs:
- serve_gate: bfloat16 [64, 2048, 1408], P('expert', None, 'shard')
- serve_up: bfloat16 [64, 2048, 1408], P('expert', None, 'shard')
- scale_gate: float32 [64, 1408], P('expert', 'shard')
- scale_up: float32 [64, 1408], P('expert', 'shard')
- serve_router: bfloat16 [2048, 64], replicated
All inputs are finite; a program needn't handle non-finite values. Where the computation divides by a largest or mean magnitude, that divisor is 1e-20 or more.
Results may differ from a plain program's by a relative error of at most 0.001.
Values may be sent and summed in bfloat16 or wider, within the bound.
A program may use at most 64 MiB of HBM per device.

v0:
```python
import jax
import jax.numpy as jnp
from jax import lax
from jax.sharding import PartitionSpec as P

D_MODEL = 2048


def split_up(shard, dim, size):
    shape = shard.shape
    parts = shard.reshape(*shape[:dim], size, shape[dim] // size, *shape[dim + 1 :])
    return jnp.moveaxis(parts, dim, 0)


def sent_and_summed(shard, axis, dim):
    parts = split_up(shard, dim, lax.axis_size(axis))
    arrived = lax.all_to_all(parts, axis, split_axis=0, concat_axis=0, tiled=True)
    return arrived.sum(axis=0)


def rows_for(lines, size):
    spare = -lines.shape[0] % size
    if not spare:
        return lines
    return jnp.concatenate([lines, jnp.zeros((spare, *lines.shape[1:]), lines.dtype)])


def in_order(parts, dim):
    shape = list(parts.shape[1:])
    shape[dim] *= parts.shape[0]
    return jnp.moveaxis(parts, 0, dim).reshape(shape)


def from_everyone(shard, axis):
    size = lax.axis_size(axis)
    return lax.all_to_all(
        jnp.broadcast_to(shard[None], (size, *shard.shape)), axis, 0, 0, tiled=True
    )


def gathered_copies(shard, axis, dim):
    return in_order(from_everyone(shard, axis), dim)


def total_of(shard, axes):
    own = sent_and_summed(rows_for(shard, lax.axis_size(axes)), axes, 0)
    whole = gathered_copies(own, axes, 0)
    return whole[: len(shard)].reshape(shard.shape)


def packed_total(arrays, axis):
    ends = [0]
    for a in arrays:
        ends.append(ends[-1] + a.size)
    total = total_of(jnp.concatenate([a.ravel() for a in arrays]), axis)
    return tuple((total[b:e].reshape(a.shape) for a, b, e in zip(arrays, ends, ends[1:])))


def in_one_piece(arrays, axis, split_dim, concat_dim, along):
    ends, at = ([], 0)
    for a in arrays[:-1]:
        at += a.shape[along]
        ends.append(at)
    both = jnp.concatenate(arrays, axis=along)
    return tuple(
        jnp.split(
            lax.all_to_all(both, axis, split_axis=split_dim, concat_axis=concat_dim, tiled=True),
            ends,
            axis=along,
        )
    )


def on_device(w_gate, w_up, router_weight, router_gain):
    total_gate, total_up = packed_total(
        (jnp.sum(jnp.abs(w_gate), axis=1), jnp.sum(jnp.abs(w_up), axis=1)), "shard"
    )
    scale_gate = total_gate / D_MODEL
    scale_up = total_up / D_MODEL
    narrow_gate, narrow_up = (
        (w_gate / jnp.expand_dims(scale_gate, 1)).astype(jnp.bfloat16),
        (w_up / jnp.expand_dims(scale_up, 1)).astype(jnp.bfloat16),
    )
    serve_gate, serve_up = in_one_piece((narrow_gate, narrow_up), "shard", 2, 1, 0)
    scale_gate = lax.dynamic_slice_in_dim(
        scale_gate, lax.axis_index("shard") * serve_gate.shape[2], serve_gate.shape[2], axis=1
    )
    scale_up = lax.dynamic_slice_in_dim(
        scale_up, lax.axis_index("shard") * serve_up.shape[2], serve_up.shape[2], axis=1
    )
    part_router = (router_weight * router_gain[:, None]).astype(jnp.bfloat16)
    row_router = gathered_copies(part_router, "shard", 0)
    serve_router = gathered_copies(row_router, "expert", 1)
    return (serve_gate, serve_up, scale_gate, scale_up, serve_router)


def solution(mesh):
    placed = (
        P("expert", "shard", None),
        P("expert", "shard", None),
        P("shard", "expert"),
        P("shard"),
    )
    return jax.shard_map(
        on_device,
        mesh=mesh,
        in_specs=placed,
        out_specs=(
            P("expert", None, "shard"),
            P("expert", None, "shard"),
            P("expert", "shard"),
            P("expert", "shard"),
            P(),
        ),
        check_vma=False,
    )
```

profile of v0, /device:TPU:1, one launch (start us, length us, event | category | flops | bytes accessed | tf_op | source)
XLA Modules:
  0.0 178.4 jit_solution(17516819587197205589)
XLA Ops:
  0.7 2.2 %abs_reduce_fusion.1 = f32[8,1408]{1,0:T(8,128)S(1)} fusion(f32[8,64,1408]{2,1,0:T(8,128)} %param.4), kind=kLoop, calls=%fused_computation.4 | loop fusion | flops 1430528 | bytes 2928640 | tf_op jit(solution)/shard_map/reduce_sum | solution.py:76
  2.9 2.3 %abs_reduce_fusion = f32[8,1408]{1,0:T(8,128)S(1)} fusion(f32[8,64,1408]{2,1,0:T(8,128)} %param.5), kind=kLoop, calls=%fused_computation.3 | loop fusion | flops 1430528 | bytes 2928640 | tf_op jit(solution)/shard_map/reduce_sum | solution.py:76
  5.3 0.7 all_to_all.27
  6.0 12.0 %all-to-all-start = ((f32[32,1,704]{2,1,0:T(1,128)}), f32[32,1,704]{2,1,0:T(1,128)S(1)}, u32[]{:S(2)}, u32[]{:S(2)}) async-start(f32[32,1,704]{2,1,0:T(1,128)} %all_to_all.27), calls=%async_computation | async-start | bytes 196608 | tf_op jit(solution)/shard_map/all_to_all | solution.py:17
  18.1 0.7 reshape.65
  18.8 8.3 %all-to-all-done = f32[32,1,704]{2,1,0:T(1,128)S(1)} async-done(((f32[32,1,704]{2,1,0:T(1,128)}), f32[32,1,704]{2,1,0:T(1,128)S(1)}, u32[]{:S(2)}, u32[]{:S(2)}) %all-to-all-start) | async-done | bytes 90144 | tf_op jit(solution)/shard_map/all_to_all | solution.py:17
  27.2 3.9 %all-to-all-start.3 = ((bf16[32,2,256]{2,1,0:T(2,128)(2,1)}), bf16[32,2,256]{2,1,0:T(2,128)(2,1)S(1)}, u32[]{:S(2)}, u32[]{:S(2)}) async-start(bf16[32,2,256]{2,1,0:T(2,128)(2,1)} %reshape.65), calls=%async_computation.3 | async-start | bytes 65536 | tf_op jit(solution)/shard_map/all_to_all | solution.py:36
  31.1 8.6 %all-to-all-done.3 = bf16[32,2,256]{2,1,0:T(2,128)(2,1)S(1)} async-done(((bf16[32,2,256]{2,1,0:T(2,128)(2,1)}), bf16[32,2,256]{2,1,0:T(2,128)(2,1)S(1)}, u32[]{:S(2)}, u32[]{:S(2)}) %all-to-all-start.3) | async-done | bytes 32800 | tf_op jit(solution)/shard_map/all_to_all | solution.py:36
  39.7 0.7 broadcast_in_dim.8
  40.3 3.9 %all-to-all-start.1 = ((f32[32,1,704]{2,1,0:T(1,128)}), f32[32,1,704]{2,1,0:T(1,128)S(1)}, u32[]{:S(2)}, u32[]{:S(2)}) async-start(f32[32,1,704]{2,1,0:T(1,128)} %broadcast_in_dim.8), calls=%async_computation.1 | async-start | bytes 196608 | tf_op jit(solution)/shard_map/all_to_all | solution.py:36
  44.2 4.1 %copy.27 = f32[8,64,1408]{1,0,2:T(8,128)} copy(f32[8,64,1408]{2,1,0:T(8,128)S(1)} %copy-done) | data formatting | bytes 5767168 | tf_op args[0]
  48.3 5.4 %copy.29 = f32[8,64,1408]{1,0,2:T(8,128)} copy(f32[8,64,1408]{2,1,0:T(8,128)} %param.5) | data formatting | bytes 5767168 | tf_op args[1]
  53.7 0.1 reshape.66
  53.8 0.1 broadcast_in_dim.10
  54.0 0.7 broadcast_in_dim.11
  54.7 8.0 %all-to-all-start.4 = ((bf16[8,2048,8]{1,2,0:T(8,128)(2,1)}), bf16[8,2048,8]{1,2,0:T(8,128)(2,1)S(1)}, u32[]{:S(2)}, u32[]{:S(2)}) async-start(bf16[8,2048,8]{1,2,0:T(8,128)(2,1)} %broadcast_in_dim.11), calls=%async_computation.4 | async-start | bytes 524288 | tf_op jit(solution)/shard_map/all_to_all | solution.py:36
  62.7 0.3 fusion.1
  63.1 0.3 copy.26
  63.4 0.3 copy.28
  63.7 6.4 %divide_convert_fusion = (bf16[8,64,1408]{1,0,2:T(8,128)(2,1)S(1)}, bf16[8,64,1408]{1,0,2:T(8,128)(2,1)S(1)}) fusion(f32[8,64,1408]{1,0,2:T(8,128)} %copy.29, f32[8,1408]{0,1:T(8,128)S(1)} %copy.28, f32[8,64,1408]{1,0,2:T(8,128)} %copy.27, f32[8,1408]{0,1:T(8,128)S(1)} %copy.26), kind=kLoop, calls=%fused_computation.1 | loop fusion | flops 2883584 | bytes 8740864 | tf_op jit(solution)/shard_map/convert_element_type | solution.py:82
  70.1 3.5 %fusion.3 = bf16[1408,16,64]{2,1,0:T(8,128)(2,1)} fusion(bf16[8,64,1408]{1,0,2:T(8,128)(2,1)S(1)} %get-tuple-element.9, bf16[8,64,1408]{1,0,2:T(8,128)(2,1)S(1)} %get-tuple-element.10), kind=kLoop, calls=%fused_computation.14 | loop fusion | flops 5767168 | bytes 5767168
  73.6 8.5 %reshape.63 = bf16[32,2,22528]{2,1,0:T(2,128)(2,1)} reshape(bf16[1408,16,64]{2,1,0:T(8,128)(2,1)} %fusion.3) | data formatting | bytes 5767168
  82.0 9.0 %all-to-all-start.2 = ((bf16[32,2,22528]{2,1,0:T(2,128)(2,1)}), bf16[32,2,22528]{2,1,0:T(2,128)(2,1)S(1)}, u32[]{:S(2)}, u32[]{:S(2)}) async-start(bf16[32,2,22528]{2,1,0:T(2,128)(2,1)} %reshape.63), calls=%async_computation.2 | async-start | bytes 5767168 | tf_op jit(solution)/shard_map/all_to_all | solution.py:67
  91.1 0.7 constant_dynamic-slice_fusion
  91.7 64.9 %all-to-all-done.2 = bf16[32,2,22528]{2,1,0:T(2,128)(2,1)S(1)} async-done(((bf16[32,2,22528]{2,1,0:T(2,128)(2,1)}), bf16[32,2,22528]{2,1,0:T(2,128)(2,1)S(1)}, u32[]{:S(2)}, u32[]{:S(2)}) %all-to-all-start.2) | async-done | bytes 2883616 | tf_op jit(solution)/shard_map/all_to_all | solution.py:67
  156.6 5.9 %reshape.64 = bf16[1408,16,64]{2,1,0:T(8,128)(2,1)} reshape(bf16[32,2,22528]{2,1,0:T(2,128)(2,1)S(1)} %all-to-all-done.2) | data formatting | bytes 5767168
  162.5 4.7 %fusion.2 = (bf16[8,32,64,44]{2,0,3,1:T(8,128)(2,1)}, bf16[8,32,64,44]{2,0,3,1:T(8,128)(2,1)S(1)}) fusion(bf16[16,32,64,44]{2,0,3,1:T(8,128)(2,1)} %bitcast.22), kind=kLoop, calls=%fused_computation.13 | loop fusion | bytes 5767168 | tf_op jit(solution)/shard_map/split | solution.py:66
  167.2 1.1 copy.30
  168.3 3.2 %split.11 = bf16[8,2048,44]{1,0,2:T(8,128)(2,1)} reshape(bf16[8,32,64,44]{2,1,0,3:T(8,128)(2,1)S(1)} %copy.30) | data formatting | bytes 2883584 | tf_op jit(solution)/shard_map/split | solution.py:66
  171.5 2.9 %copy.31 = bf16[8,32,64,44]{2,1,0,3:T(8,128)(2,1)S(1)} copy(bf16[8,32,64,44]{2,0,3,1:T(8,128)(2,1)} %get-tuple-element.7) | data formatting | bytes 2883584 | tf_op jit(solution)/shard_map/split | solution.py:66
  174.5 3.2 %split.13 = bf16[8,2048,44]{1,0,2:T(8,128)(2,1)} reshape(bf16[8,32,64,44]{2,1,0,3:T(8,128)(2,1)S(1)} %copy.31) | data formatting | bytes 2883584 | tf_op jit(solution)/shard_map/split | solution.py:66
  177.7 0.7 copy.34
  (17 shorter events, 0.4 us)
Async XLA Ops:
  0.6 17.4 %copy-start.1 = (f32[64,8]{0,1:T(8,128)S(1)}, f32[64,8]{0,1:T(8,128)}, u32[]{:S(2)}) copy-start(f32[64,8]{0,1:T(8,128)} %param.6) | copy-start | bytes 6148
  0.6 17.4 %copy-start.2 = (f32[64]{0:T(128)S(1)}, f32[64]{0:T(128)}, u32[]{:S(2)}) copy-start(f32[64]{0:T(128)} %param.7) | copy-start | bytes 772
  2.8 41.4 %copy-start = (f32[8,64,1408]{2,1,0:T(8,128)S(1)}, f32[8,64,1408]{2,1,0:T(8,128)}, u32[]{:S(2)}) copy-start(f32[8,64,1408]{2,1,0:T(8,128)} %param.4) | copy-start | bytes 8650756
  6.0 21.2 %all-to-all-start = ((f32[32,1,704]{2,1,0:T(1,128)}), f32[32,1,704]{2,1,0:T(1,128)S(1)}, u32[]{:S(2)}, u32[]{:S(2)}) async-start(f32[32,1,704]{2,1,0:T(1,128)} %all_to_all.27), calls=%async_computation | async-start | bytes 196608 | tf_op jit(solution)/shard_map/all_to_all | solution.py:17
  27.2 12.5 %all-to-all-start.3 = ((bf16[32,2,256]{2,1,0:T(2,128)(2,1)}), bf16[32,2,256]{2,1,0:T(2,128)(2,1)S(1)}, u32[]{:S(2)}, u32[]{:S(2)}) async-start(bf16[32,2,256]{2,1,0:T(2,128)(2,1)} %reshape.65), calls=%async_computation.3 | async-start | bytes 65536 | tf_op jit(solution)/shard_map/all_to_all | solution.py:36
  40.3 13.6 %all-to-all-start.1 = ((f32[32,1,704]{2,1,0:T(1,128)}), f32[32,1,704]{2,1,0:T(1,128)S(1)}, u32[]{:S(2)}, u32[]{:S(2)}) async-start(f32[32,1,704]{2,1,0:T(1,128)} %broadcast_in_dim.8), calls=%async_computation.1 | async-start | bytes 196608 | tf_op jit(solution)/shard_map/all_to_all | solution.py:36
  54.7 27.3 %all-to-all-start.4 = ((bf16[8,2048,8]{1,2,0:T(8,128)(2,1)}), bf16[8,2048,8]{1,2,0:T(8,128)(2,1)S(1)}, u32[]{:S(2)}, u32[]{:S(2)}) async-start(bf16[8,2048,8]{1,2,0:T(8,128)(2,1)} %broadcast_in_dim.11), calls=%async_computation.4 | async-start | bytes 524288 | tf_op jit(solution)/shard_map/all_to_all | solution.py:36
  82.0 74.5 %all-to-all-start.2 = ((bf16[32,2,22528]{2,1,0:T(2,128)(2,1)}), bf16[32,2,22528]{2,1,0:T(2,128)(2,1)S(1)}, u32[]{:S(2)}, u32[]{:S(2)}) async-start(bf16[32,2,22528]{2,1,0:T(2,128)(2,1)} %reshape.63), calls=%async_computation.2 | async-start | bytes 5767168 | tf_op jit(solution)/shard_map/all_to_all | solution.py:67
where the time goes:
time: 181 us; the launch traced here: 178 us
  waiting for transfers between devices  81.8 us (45%)
  local copies, waits for them, and re-layouts  44.4 us (25%)
  starting transfers between devices  36.7 us (20%)
  other arithmetic  14.7 us (8%)
    all_to_all x1, waiting for transfers between devices, in_one_piece(): lax.all_to_all(both, axis, split_axis=split_dim, concat_axis=concat_dim,...  64.9 us
    unnamed x14, local copies, waits for them, and re-layouts  25.5 us
    all_to_all x3, starting transfers between devices, from_everyone(): lax.all_to_all(jnp.broadcast_to(shard[None], (size, *shard.shape)), axis,...  15.7 us
    split x5, local copies, waits for them, and re-layouts, in_one_piece(): jnp.split(lax.all_to_all(both, axis, split_axis=split_dim, concat_axis=co...  15.1 us
    all_to_all x1, starting transfers between devices, sent_and_summed(): lax.all_to_all(parts, axis, split_axis=0, concat_axis=0, tiled=True)  12 us
    all_to_all x1, starting transfers between devices, in_one_piece(): lax.all_to_all(both, axis, split_axis=split_dim, concat_axis=concat_dim,...  9 us
    all_to_all x3, waiting for transfers between devices, from_everyone(): lax.all_to_all(jnp.broadcast_to(shard[None], (size, *shard.shape)), axis,...  8.56 us
    all_to_all x1, waiting for transfers between devices, sent_and_summed(): lax.all_to_all(parts, axis, split_axis=0, concat_axis=0, tiled=True)  8.34 us
  transfers between devices with their start and end apart: 5, of which 3 were waited for; matrix products, arithmetic and copies ran while one was open for 17% of the time, Pallas kernels for 0%

commit v1 on v0

v1 whole, which is shorter than its diff:
```python
import functools

import jax
import jax.numpy as jnp
from jax import lax
from jax.experimental import pallas as pl
from jax.experimental.pallas import tpu as pltpu
from jax.sharding import PartitionSpec as P

MESH = pl.DeviceIdType.MESH
Z, Y = 8, 4
N = Z * Y
GROUPS = 8
E, ROWS, COLS = 8, 64, 1408
D_MODEL = N * ROWS
OWN = COLS // N
PAD = 48
LANES = 128
TILES = COLS // LANES
GROUP = Y * OWN


def tile(t):
    m, c = t // TILES, t % TILES
    return (
        pl.ds(pl.multiple_of(m * 8, 8), 8),
        pl.ds(pl.multiple_of(c * LANES, LANES), LANES),
    )


def pick_from(i, values):
    chosen = values[0]
    for at, value in enumerate(values[1:], 1):
        chosen = jnp.where(i == at, value, chosen)
    return chosen


def owner(t):
    m, c = t // TILES, t % TILES
    group = (c * LANES + LANES // 2) // GROUP
    second = jnp.where((c == 2) | (c == 6) | (c == 9), 1, 0)
    return lax.rem(group + Z // 2, Z) * Y + 2 * m + second


def tile_of(device):
    group, y = lax.rem(device // Y + Z // 2, Z), lax.rem(device, Y)
    m, second = y // 2, y % 2
    two = (group == 1) | (group == 4) | (group == 6)
    return m * TILES + pick_from(group, (0, 1, 3, 4, 5, 7, 8, 10)) + second, two | (second == 0)


def tiles_of(group):
    return group * GROUP // LANES, (group * GROUP + GROUP - 1) // LANES


def window(j):
    first, last = tiles_of(j // Y)
    base = jnp.minimum(jnp.maximum(j * OWN // LANES, first), last - 1)
    return base, j * OWN - base * LANES


def kernel(
    wg_ref, wu_ref, rw_hbm, gain_hbm,
    og_ref, ou_ref, sg_ref, su_ref, or_ref,
    w, rw, gain, part, sums, total, q, tmp, send, recv, rt, rts, row,
    load_sem, small_sem, rs_send, rs_recv, ag_send, ag_recv, rt_send, rt_recv, x_send, x_recv,
    send_sem, recv_sem,
):
    me = lax.axis_index("shard")
    ex = lax.axis_index("expert")
    z, y = me // Y, me % Y
    mine, owns = tile_of(me)

    def offset(i):
        g = i // Y
        dz = jnp.where(g % 2 == 1, (7 - g) // 2, 4 + g // 2)
        return dz, lax.rem(i + 1, Y)

    def peer(k):
        dz, dy = offset(k - 1)
        return lax.rem(z + dz, Z) * Y + lax.rem(y + dy, Y)

    def across(k):
        return lax.rem(ex + k, GROUPS)

    def loads(m, e):
        ref = wg_ref if m == 0 else wu_ref
        return pltpu.make_async_copy(ref.at[e], w.at[m, e], load_sem.at[m * E + e])

    barrier = pltpu.get_barrier_semaphore()

    def greet(k, _):
        pl.semaphore_signal(barrier, inc=1, device_id={"shard": peer(k)}, device_id_type=MESH)
        return 0

    def greet_across(k, _):
        pl.semaphore_signal(barrier, inc=1, device_id={"expert": across(k)}, device_id_type=MESH)
        return 0

    for m in range(2):
        for e in range(E):
            loads(m, e).start()
    small = (
        pltpu.make_async_copy(rw_hbm, rw, small_sem.at[0]),
        pltpu.make_async_copy(gain_hbm, gain, small_sem.at[1]),
    )
    for copy in small:
        copy.start()
    lax.fori_loop(1, N, greet, 0)
    lax.fori_loop(1, GROUPS, greet_across, 0)

    for copy in small:
        copy.wait()
    routed = (rw[...] * gain[...]).astype(jnp.bfloat16)
    rt[...] = jnp.concatenate([routed, routed], axis=1)

    def sum_of(m):
        def body(e, _):
            pltpu.make_async_copy(wg_ref.at[e], w.at[m, e], load_sem.at[m * E + e]).wait()
            acc = jnp.abs(w[m, e, 0:8, :])
            for g in range(1, ROWS // 8):
                acc = acc + jnp.abs(w[m, e, g * 8 : g * 8 + 8, :])
            part[pl.ds(m * 8 + e, 1), :] = jnp.sum(acc, axis=0, keepdims=True)
            return 0

        lax.fori_loop(0, E, body, 0)

    def rs(k):
        to = peer(k)
        t, has = tile_of(to)
        return has, lambda: pltpu.make_async_remote_copy(
            src_ref=part.at[tile(t)], dst_ref=sums.at[k], send_sem=rs_send.at[k],
            recv_sem=rs_recv.at[k], device_id={"shard": to}, device_id_type=MESH,
        )

    def rs_wait(k):
        pltpu.make_async_copy(sums.at[0], sums.at[k], rs_recv.at[k]).wait()

    def ag(k):
        return pltpu.make_async_remote_copy(
            src_ref=total.at[tile(mine)], dst_ref=total.at[tile(mine)], send_sem=ag_send.at[k],
            recv_sem=ag_recv.at[mine], device_id={"shard": peer(N - k)}, device_id_type=MESH,
        )

    def router(k):
        return pltpu.make_async_remote_copy(
            src_ref=rt, dst_ref=rts.at[me], send_sem=rt_send.at[k],
            recv_sem=rt_recv.at[me], device_id={"shard": peer(k)}, device_id_type=MESH,
        )

    def router_across(k):
        return pltpu.make_async_remote_copy(
            src_ref=row, dst_ref=or_ref.at[ex], send_sem=x_send.at[k],
            recv_sem=x_recv.at[ex], device_id={"expert": across(k)}, device_id_type=MESH,
        )

    sum_of(0)
    sum_of(1)
    pl.semaphore_wait(barrier, N - 1 + GROUPS - 1)

    def rs_start(k, _):
        has, copy = rs(k)

        @pl.when(has)
        def _():
            copy().start()

        return 0

    lax.fori_loop(1, N, rs_start, 0)
    lax.fori_loop(1, N, lambda k, _: (router(k).start(), 0)[1], 0)

    @pl.when(owns)
    def _():
        def add(k, acc):
            rs_wait(k)
            return acc + sums[k]

        total[tile(mine)] = lax.fori_loop(1, N, add, part[tile(mine)])
        lax.fori_loop(1, N, lambda k, _: (ag(k).start(), 0)[1], 0)

    def scale_tile(c, _):
        cols = pl.ds(pl.multiple_of(c * LANES, LANES), LANES)
        for m in range(2):
            t = m * TILES + c

            @pl.when(owner(t) != me)
            def _():
                pltpu.make_async_copy(part.at[tile(t)], total.at[tile(t)], ag_recv.at[t]).wait()

            inv = D_MODEL / total[m * 8 : m * 8 + 8, cols]
            for e in range(E):
                q[e, m * ROWS : (m + 1) * ROWS, cols] = (
                    w[m, e, :, cols] * inv[e : e + 1, :]
                ).astype(jnp.bfloat16)
        return 0

    def bulk(i):
        to = peer(i + 1)
        return to, lambda: pltpu.make_async_remote_copy(
            src_ref=send.at[to], dst_ref=recv.at[me], send_sem=send_sem.at[i],
            recv_sem=recv_sem.at[me], device_id={"shard": to}, device_id_type=MESH,
        )

    def pack(j):
        base, shift = window(j)
        at = lax.broadcasted_iota(jnp.int32, (PAD, 2 * LANES), 0) + shift
        pick = (at == lax.broadcasted_iota(jnp.int32, (PAD, 2 * LANES), 1)).astype(jnp.float32)
        pick = pick.astype(jnp.bfloat16)
        cols = pl.ds(pl.multiple_of(base * LANES, LANES), 2 * LANES)
        for e in range(E):
            tmp[pl.ds(e, PAD, stride=8), :] = lax.dot_general(
                pick, q[e, :, cols], (((1,), (1,)), ((), ())), preferred_element_type=jnp.float32
            )
        send[j] = tmp[0 : OWN * 8, :].reshape(OWN, 8, LANES).astype(jnp.bfloat16)

    def send_group(step, _):
        group = lax.rem(z + offset(step * Y)[0], Z)
        first, last = tiles_of(group)
        below = ((step % 2 == 0) & (step > 0)) | (step == Z - 1)
        above = step % 2 == 1
        first = first + jnp.where(below & (group > 0), 1, 0)
        last = last - jnp.where(above & (group < Z - 1), 1, 0)
        lax.fori_loop(first, last + 1, scale_tile, 0)

        def send_one(i, _):
            to, copy = bulk(i)
            pack(to)

            @pl.when(i < N - 1)
            def _():
                copy().start()

            return 0

        lax.fori_loop(step * Y, step * Y + Y, send_one, 0)
        return 0

    lax.fori_loop(0, Z, send_group, 0)
    own = pltpu.make_async_copy(send.at[me], recv.at[me], recv_sem.at[me])
    own.start()

    base, shift = window(me)
    for m, ref in enumerate((sg_ref, su_ref)):
        rows = pl.ds(m * 8, 8)
        pair = total[rows, pl.ds(pl.multiple_of(base * LANES, LANES), 2 * LANES)]
        ref[...] = pltpu.roll(pair, 2 * LANES - shift, 1)[:, :OWN] / D_MODEL

    low = lax.broadcasted_iota(jnp.int32, (8, LANES), 1) < ROWS
    rts[me] = rt[...]

    def rt_wait(s, _):
        @pl.when(s != me)
        def _():
            pltpu.make_async_remote_copy(
                src_ref=rt, dst_ref=rts.at[s], send_sem=rt_send.at[0],
                recv_sem=rt_recv.at[s], device_id={"shard": me}, device_id_type=MESH,
            ).wait_recv()

        return 0

    lax.fori_loop(0, N, rt_wait, 0)
    for p in range(N // 2):
        a, b = rts[2 * p].astype(jnp.float32), rts[2 * p + 1].astype(jnp.float32)
        row[:, p * LANES : (p + 1) * LANES] = jnp.where(low, a, b).astype(jnp.bfloat16)
    lax.fori_loop(1, GROUPS, lambda k, _: (router_across(k).start(), 0)[1], 0)
    own_row = pltpu.make_async_copy(row, or_ref.at[ex], x_recv.at[ex])
    own_row.start()

    def merge(i, _):
        g = i // 2
        dz = jnp.where(g % 2 == 1, (7 - g) // 2, 4 + g // 2)
        p = lax.rem(z - dz + Z, Z) * 2 + i % 2
        for h in range(2):
            s = 2 * p + h
            pltpu.make_async_copy(send.at[s], recv.at[s], recv_sem.at[s]).wait()
        a, b = recv[2 * p], recv[2 * p + 1]
        lanes = pl.ds(pl.multiple_of(p * LANES, LANES), LANES)
        og_ref[:, :, lanes] = jnp.concatenate([a[..., :ROWS], b[..., :ROWS]], axis=-1)
        ou_ref[:, :, lanes] = jnp.concatenate([a[..., ROWS:], b[..., ROWS:]], axis=-1)
        return 0

    lax.fori_loop(0, N // 2, merge, 0)

    def drain(i, _):
        bulk(i)[1]().wait_send()
        router(i + 1).wait_send()
        has, copy = rs(i + 1)

        @pl.when(has)
        def _():
            copy().wait_send()

        @pl.when(owns)
        def _():
            ag(i + 1).wait_send()

        return 0

    lax.fori_loop(0, N - 1, drain, 0)
    lax.fori_loop(1, GROUPS, lambda k, _: (router_across(k).wait_send(), 0)[1], 0)

    def x_wait(k, _):
        pltpu.make_async_copy(row, or_ref.at[k], x_recv.at[k]).wait()
        return 0

    lax.fori_loop(0, GROUPS, x_wait, 0)


def put_out(*refs):
    ins, outs, sem = refs[:5], refs[5:10], refs[10]
    copies = [pltpu.make_async_copy(a, b, sem.at[i]) for i, (a, b) in enumerate(zip(ins, outs))]
    for copy in copies:
        copy.start()
    for copy in copies:
        copy.wait()


def on_device(w_gate, w_up, router_weight, router_gain):
    any_ = pl.BlockSpec(memory_space=pl.ANY)
    hbm = pl.BlockSpec(memory_space=pltpu.HBM)
    vmem = pl.BlockSpec(memory_space=pltpu.VMEM)
    dma = pltpu.SemaphoreType.DMA
    bf16, f32 = jnp.bfloat16, jnp.float32
    results = (
        jax.ShapeDtypeStruct((OWN, E, D_MODEL), bf16),
        jax.ShapeDtypeStruct((OWN, E, D_MODEL), bf16),
        jax.ShapeDtypeStruct((E, OWN), f32),
        jax.ShapeDtypeStruct((E, OWN), f32),
        jax.ShapeDtypeStruct((GROUPS, 8, D_MODEL), bf16),
    )
    held = pl.pallas_call(
        kernel,
        out_shape=results,
        in_specs=[hbm] * 4,
        out_specs=(vmem,) * 5,
        scratch_shapes=[
            pltpu.VMEM((2, E, ROWS, COLS), f32),
            pltpu.VMEM((8, ROWS), f32),
            pltpu.VMEM((1, ROWS), f32),
            pltpu.VMEM((16, COLS), f32),
            pltpu.VMEM((N, 8, LANES), f32),
            pltpu.VMEM((16, COLS), f32),
            pltpu.VMEM((E, 2 * ROWS, COLS), bf16),
            pltpu.VMEM((PAD * 8, LANES), f32),
            pltpu.VMEM((N, OWN, 8, LANES), bf16),
            pltpu.VMEM((N, OWN, 8, LANES), bf16),
            pltpu.VMEM((8, LANES), bf16),
            pltpu.VMEM((N, 8, LANES), bf16),
            pltpu.VMEM((8, D_MODEL), bf16),
            dma((2 * E,)), dma((2,)), dma((N,)), dma((N,)), dma((N,)), dma((N,)), dma((N,)), dma((N,)),
            dma((GROUPS,)), dma((GROUPS,)), dma((N,)), dma((N,)),
        ],
        compiler_params=pltpu.CompilerParams(
            collective_id=0, has_side_effects=True, vmem_limit_bytes=48 << 20
        ),
    )(*(
        pltpu.with_memory_space_constraint(x, pltpu.HBM)
        for x in (w_gate, w_up, router_weight.T, router_gain[None, :])
    ))
    gate, up, scale_gate, scale_up, router = pl.pallas_call(
        put_out,
        out_shape=results,
        in_specs=[any_] * 5,
        out_specs=(any_,) * 5,
        scratch_shapes=[dma((5,))],
    )(*(pltpu.with_memory_space_constraint(x, pltpu.VMEM) for x in held))
    return (
        gate.transpose(1, 2, 0),
        up.transpose(1, 2, 0),
        scale_gate,
        scale_up,
        router.reshape(GROUPS * 8, D_MODEL).T,
    )


def solution(mesh):
    placed = (
        P("expert", "shard", None),
        P("expert", "shard", None),
        P("shard", "expert"),
        P("shard"),
    )
    return jax.shard_map(
        on_device,
        mesh=mesh,
        in_specs=placed,
        out_specs=(
            P("expert", None, "shard"),
            P("expert", None, "shard"),
            P("expert", "shard"),
            P("expert", "shard"),
            P(),
        ),
        check_vma=False,
    )
```

time: 181 us -> 93.2 us (0.51); the launches traced: 178 us -> 93.1 us
  Pallas kernels: 0 us -> 92.5 us
  waiting for transfers between devices: 81.8 us -> 0 us
  local copies, waits for them, and re-layouts: 44.4 us -> 0 us
  starting transfers between devices: 36.7 us -> 0 us
  other arithmetic: 14.7 us -> 0 us
    pallas_call x0 -> x2, Pallas kernels: none -> 92.5 us  [the longest x1 90.8 us: on_device(): pl.pallas_call(kernel, out_shape=results, in_specs=[hbm] * 4, out_specs=(...]
    all_to_all x5 -> x0, waiting for transfers between devices: 81.8 us -> none  [the longest x1 64.9 us: in_one_piece(): lax.all_to_all(both, axis, split_axis=split_dim, concat_axis=concat_dim,...]
    all_to_all x5 -> x0, starting transfers between devices: 36.7 us -> none  [the longest x3 15.7 us: from_everyone(): lax.all_to_all(jnp.broadcast_to(shard[None], (size, *shard.shape)), axis,...]
    unnamed x14 -> x0, local copies, waits for them, and re-layouts: 25.5 us -> none
    split x5 -> x0, local copies, waits for them, and re-layouts: 15.1 us -> none  [in_one_piece(): jnp.split(lax.all_to_all(both, axis, split_axis=split_dim, concat_axis=co...]
    convert_element_type x2 -> x0, other arithmetic: 6.37 us -> none  [the longest x1 6.36 us: on_device(): (w_up / jnp.expand_dims(scale_up, 1)).astype(jnp.bfloat16)]
    reduce_sum x3 -> x0, other arithmetic: 4.54 us -> none  [the longest x1 2.3 us: on_device(): jnp.sum(jnp.abs(w_up), axis=1)]
    unnamed x1 -> x0, other arithmetic: 3.5 us -> none
  transfers between devices with their start and end apart: 5 -> 0, of which waited for: 3 -> 0; matrix products, arithmetic and copies ran while one was open for 17% -> 0% of each run, Pallas kernels for 0% -> 0%
where the time goes in v1:
time: 93.2 us; the launch traced here: 93.1 us
  Pallas kernels  92.5 us (99%)
    pallas_call x1, Pallas kernels, on_device(): pl.pallas_call(kernel, out_shape=results, in_specs=[hbm] * 4, out_specs=(...  90.8 us

profile of v1, /device:TPU:1, one launch (start us, length us, event | category | flops | bytes accessed | tf_op | source)
XLA Modules:
  0.0 93.1 jit_solution(7885209957397786111)
XLA Ops:
  0.6 90.8 %shard_map.83 = (bf16[44,8,2048]{2,1,0:T(8,128)(2,1)S(1)}, bf16[44,8,2048]{2,1,0:T(8,128)(2,1)S(1)}, f32[8,44]{1,0:T(8,128)S(1)}, f32[8,44]{1,0:T(8,128)S(1)}, bf16[8,8,2048]{2,1,0:T(8,128)(2,1)S(1)}) custom-call(f32[8,64,1408]{2,1,0:T(8,128)} %wg_ref.1, f32[8,64,1408]{2,1,0:T(8,128)} %wu_ref.1, f32[8,64]{1,0:T(8,128)} %bitcast.7, f32[1,64]{1,0:T(1,128)} %bitcast.8), custom_call_target="tpu_custom_call" | custom-call | tf_op jit(solution)/shard_map/pallas_call | solution.py:332
  91.4 1.7 %shard_map.84 = (bf16[44,8,2048]{2,1,0:T(8,128)(2,1)}, bf16[44,8,2048]{2,1,0:T(8,128)(2,1)}, f32[8,44]{1,0:T(8,128)}, f32[8,44]{1,0:T(8,128)}, bf16[8,8,2048]{2,1,0:T(8,128)(2,1)}) custom-call(bf16[44,8,2048]{2,1,0:T(8,128)(2,1)S(1)} %get-tuple-element.15.refs_0_, bf16[44,8,2048]{2,1,0:T(8,128)(2,1)S(1)} %get-tuple-element.16.refs_1_, ...), custom_call_target="tpu_custom_call" | custom-call | tf_op jit(solution)/shard_map/pallas_call | solution.py:361

commit v2 on v1

--- a/solution.py
+++ b/solution.py
@@ -14,7 +14,7 @@
 E, ROWS, COLS = 8, 64, 1408
 D_MODEL = N * ROWS
 OWN = COLS // N
-PAD = 48
+HALF, PAD = OWN // 2, 24
 LANES = 128
 TILES = COLS // LANES
 GROUP = Y * OWN
@@ -154,20 +154,23 @@
             recv_sem=x_recv.at[ex], device_id={"expert": across(k)}, device_id_type=MESH,
         )
 
+    def rs_start(m):
+        def body(k, _):
+            has, copy = rs(k)
+
+            @pl.when(has & (tile_of(peer(k))[0] // TILES == m))
+            def _():
+                copy().start()
+
+            return 0
+
+        lax.fori_loop(1, N, body, 0)
+
     sum_of(0)
+    pl.semaphore_wait(barrier, N - 1 + GROUPS - 1)
+    rs_start(0)
     sum_of(1)
-    pl.semaphore_wait(barrier, N - 1 + GROUPS - 1)
-
-    def rs_start(k, _):
-        has, copy = rs(k)
-
-        @pl.when(has)
-        def _():
-            copy().start()
-
-        return 0
-
-    lax.fori_loop(1, N, rs_start, 0)
+    rs_start(1)
     lax.fori_loop(1, N, lambda k, _: (router(k).start(), 0)[1], 0)
 
     @pl.when(owns)
@@ -179,53 +182,71 @@
         total[tile(mine)] = lax.fori_loop(1, N, add, part[tile(mine)])
         lax.fori_loop(1, N, lambda k, _: (ag(k).start(), 0)[1], 0)
 
-    def scale_tile(c, _):
+    def scale_tile(m, c):
         cols = pl.ds(pl.multiple_of(c * LANES, LANES), LANES)
-        for m in range(2):
-            t = m * TILES + c
-
-            @pl.when(owner(t) != me)
-            def _():
-                pltpu.make_async_copy(part.at[tile(t)], total.at[tile(t)], ag_recv.at[t]).wait()
-
-            inv = D_MODEL / total[m * 8 : m * 8 + 8, cols]
-            for e in range(E):
-                q[e, m * ROWS : (m + 1) * ROWS, cols] = (
-                    w[m, e, :, cols] * inv[e : e + 1, :]
-                ).astype(jnp.bfloat16)
-        return 0
-
-    def bulk(i):
-        to = peer(i + 1)
+        t = m * TILES + c
+
+        @pl.when(owner(t) != me)
+        def _():
+            pltpu.make_async_copy(part.at[tile(t)], total.at[tile(t)], ag_recv.at[t]).wait()
+
+        inv = D_MODEL / total[m * 8 : m * 8 + 8, cols]
+        for e in range(E):
+            q[m, e * ROWS : (e + 1) * ROWS, cols] = (
+                w[m, e, :, cols] * inv[e : e + 1, :]
+            ).astype(jnp.bfloat16)
+
+    def order(i):
+        early = i < 3 * Y
+        j = i - 3 * Y
+        dz = jnp.where(early, pick_from(i % 3, (3, 5, 4)), pick_from(j % 5, (2, 6, 1, 7, 0)))
+        return dz, pick_from(jnp.where(early, i // 3, j // 5), (1, 3, 2, 0))
+
+    def bulk(m, i):
+        dz, dy = order(i)
+        to = lax.rem(z + dz, Z) * Y + lax.rem(y + dy, Y)
         return to, lambda: pltpu.make_async_remote_copy(
-            src_ref=send.at[to], dst_ref=recv.at[me], send_sem=send_sem.at[i],
-            recv_sem=recv_sem.at[me], device_id={"shard": to}, device_id_type=MESH,
-        )
-
-    def pack(j):
+            src_ref=send.at[m, to], dst_ref=recv.at[m, me], send_sem=send_sem.at[m, i],
+            recv_sem=recv_sem.at[m, me], device_id={"shard": to}, device_id_type=MESH,
+        )
+
+    def select(first, x):
+        at = lax.broadcasted_iota(jnp.int32, (PAD, 2 * LANES), 0) + first
+        pick = (at == lax.broadcasted_iota(jnp.int32, (PAD, 2 * LANES), 1)).astype(jnp.float32)
+        return lax.dot_general(
+            pick.astype(jnp.bfloat16), x, (((1,), (1,)), ((), ())), preferred_element_type=jnp.float32
+        )
+
+    def pack(m, j):
         base, shift = window(j)
-        at = lax.broadcasted_iota(jnp.int32, (PAD, 2 * LANES), 0) + shift
-        pick = (at == lax.broadcasted_iota(jnp.int32, (PAD, 2 * LANES), 1)).astype(jnp.float32)
-        pick = pick.astype(jnp.bfloat16)
         cols = pl.ds(pl.multiple_of(base * LANES, LANES), 2 * LANES)
-        for e in range(E):
-            tmp[pl.ds(e, PAD, stride=8), :] = lax.dot_general(
-                pick, q[e, :, cols], (((1,), (1,)), ((), ())), preferred_element_type=jnp.float32
-            )
-        send[j] = tmp[0 : OWN * 8, :].reshape(OWN, 8, LANES).astype(jnp.bfloat16)
-
-    def send_group(step, _):
-        group = lax.rem(z + offset(step * Y)[0], Z)
-        first, last = tiles_of(group)
-        below = ((step % 2 == 0) & (step > 0)) | (step == Z - 1)
-        above = step % 2 == 1
-        first = first + jnp.where(below & (group > 0), 1, 0)
-        last = last - jnp.where(above & (group < Z - 1), 1, 0)
-        lax.fori_loop(first, last + 1, scale_tile, 0)
-
-        def send_one(i, _):
-            to, copy = bulk(i)
-            pack(to)
+        for k in range(2):
+            x = q[m, k * 4 * ROWS : (k + 1) * 4 * ROWS, cols]
+            low, high = select(shift, x), select(shift + HALF, x)
+            for e in range(4):
+                lanes = slice(e * ROWS, (e + 1) * ROWS)
+                tmp[pl.ds(4 * k + e, PAD, stride=8), :] = jnp.concatenate(
+                    [low[:, lanes], high[:, lanes]], axis=1
+                )
+        send[m, j] = tmp[0 : HALF * 8, :].reshape(HALF, 8, LANES).astype(jnp.bfloat16)
+
+    def group_ready(m):
+        def body(step, _):
+            group = lax.rem(z + offset(step * Y)[0], Z)
+            first, last = tiles_of(group)
+            below = ((step % 2 == 0) & (step > 0)) | (step == Z - 1)
+            above = step % 2 == 1
+            first = first + jnp.where(below & (group > 0), 1, 0)
+            last = last - jnp.where(above & (group < Z - 1), 1, 0)
+            lax.fori_loop(first, last + 1, lambda c, _: (scale_tile(m, c), 0)[1], 0)
+            return 0
+
+        return body
+
+    def send_one(m):
+        def body(i, _):
+            to, copy = bulk(m, i)
+            pack(m, to)
 
             @pl.when(i < N - 1)
             def _():
@@ -233,12 +254,13 @@
 
             return 0
 
-        lax.fori_loop(step * Y, step * Y + Y, send_one, 0)
-        return 0
-
-    lax.fori_loop(0, Z, send_group, 0)
-    own = pltpu.make_async_copy(send.at[me], recv.at[me], recv_sem.at[me])
-    own.start()
+        return body
+
+    for m in range(2):
+        for start, end in ((0, 3), (3, Z)):
+            lax.fori_loop(start, end, group_ready(m), 0)
+            lax.fori_loop(start * Y, end * Y, send_one(m), 0)
+        pltpu.make_async_copy(send.at[m, me], recv.at[m, me], recv_sem.at[m, me]).start()
 
     base, shift = window(me)
     for m, ref in enumerate((sg_ref, su_ref)):
@@ -267,23 +289,26 @@
     own_row = pltpu.make_async_copy(row, or_ref.at[ex], x_recv.at[ex])
     own_row.start()
 
-    def merge(i, _):
-        g = i // 2
-        dz = jnp.where(g % 2 == 1, (7 - g) // 2, 4 + g // 2)
-        p = lax.rem(z - dz + Z, Z) * 2 + i % 2
-        for h in range(2):
-            s = 2 * p + h
-            pltpu.make_async_copy(send.at[s], recv.at[s], recv_sem.at[s]).wait()
-        a, b = recv[2 * p], recv[2 * p + 1]
-        lanes = pl.ds(pl.multiple_of(p * LANES, LANES), LANES)
-        og_ref[:, :, lanes] = jnp.concatenate([a[..., :ROWS], b[..., :ROWS]], axis=-1)
-        ou_ref[:, :, lanes] = jnp.concatenate([a[..., ROWS:], b[..., ROWS:]], axis=-1)
-        return 0
-
-    lax.fori_loop(0, N // 2, merge, 0)
+    def merge(m, out):
+        def body(i, _):
+            p = lax.rem(z - offset(i * 2)[0] + Z, Z) * 2 + i % 2
+            for h in range(2):
+                s = 2 * p + h
+                pltpu.make_async_copy(send.at[m, s], recv.at[m, s], recv_sem.at[m, s]).wait()
+            a, b = recv[m, 2 * p], recv[m, 2 * p + 1]
+            lanes = pl.ds(pl.multiple_of(p * LANES, LANES), LANES)
+            out[0:HALF, :, lanes] = jnp.concatenate([a[..., :ROWS], b[..., :ROWS]], axis=-1)
+            out[HALF:OWN, :, lanes] = jnp.concatenate([a[..., ROWS:], b[..., ROWS:]], axis=-1)
+            return 0
+
+        return body
+
+    lax.fori_loop(0, N // 2, merge(0, og_ref), 0)
+    lax.fori_loop(0, N // 2, merge(1, ou_ref), 0)
 
     def drain(i, _):
-        bulk(i)[1]().wait_send()
+        bulk(0, i)[1]().wait_send()
+        bulk(1, i)[1]().wait_send()
         router(i + 1).wait_send()
         has, copy = rs(i + 1)
 
@@ -341,15 +366,15 @@
             pltpu.VMEM((16, COLS), f32),
             pltpu.VMEM((N, 8, LANES), f32),
             pltpu.VMEM((16, COLS), f32),
-            pltpu.VMEM((E, 2 * ROWS, COLS), bf16),
+            pltpu.VMEM((2, E * ROWS, COLS), bf16),
             pltpu.VMEM((PAD * 8, LANES), f32),
-            pltpu.VMEM((N, OWN, 8, LANES), bf16),
-            pltpu.VMEM((N, OWN, 8, LANES), bf16),
+            pltpu.VMEM((2, N, HALF, 8, LANES), bf16),
+            pltpu.VMEM((2, N, HALF, 8, LANES), bf16),
             pltpu.VMEM((8, LANES), bf16),
             pltpu.VMEM((N, 8, LANES), bf16),
             pltpu.VMEM((8, D_MODEL), bf16),
             dma((2 * E,)), dma((2,)), dma((N,)), dma((N,)), dma((N,)), dma((N,)), dma((N,)), dma((N,)),
-            dma((GROUPS,)), dma((GROUPS,)), dma((N,)), dma((N,)),
+            dma((GROUPS,)), dma((GROUPS,)), dma((2, N)), dma((2, N)),
         ],
         compiler_params=pltpu.CompilerParams(
             collective_id=0, has_side_effects=True, vmem_limit_bytes=48 << 20

time: 93.2 us -> 91.7 us (0.984)
  Pallas kernels: 92.5 us -> 90.9 us
    pallas_call x1, Pallas kernels: 90.8 us -> 89.2 us  [on_device(): pl.pallas_call(kernel, out_shape=results, in_specs=[hbm] * 4, out_specs=(...]
where the time goes in v2:
time: 91.7 us; the launch traced here: 91.5 us
  Pallas kernels  90.9 us (99%)
    pallas_call x1, Pallas kernels, on_device(): pl.pallas_call(kernel, out_shape=results, in_specs=[hbm] * 4, out_specs=(...  89.2 us

profile of v2, /device:TPU:1, one launch (start us, length us, event | category | flops | bytes accessed | tf_op | source)
XLA Modules:
  0.0 91.5 jit_solution(7589675067237675612)
XLA Ops:
  0.6 89.2 %shard_map.83 = (bf16[44,8,2048]{2,1,0:T(8,128)(2,1)S(1)}, bf16[44,8,2048]{2,1,0:T(8,128)(2,1)S(1)}, f32[8,44]{1,0:T(8,128)S(1)}, f32[8,44]{1,0:T(8,128)S(1)}, bf16[8,8,2048]{2,1,0:T(8,128)(2,1)S(1)}) custom-call(f32[8,64,1408]{2,1,0:T(8,128)} %wg_ref.1, f32[8,64,1408]{2,1,0:T(8,128)} %wu_ref.1, f32[8,64]{1,0:T(8,128)} %bitcast.7, f32[1,64]{1,0:T(1,128)} %bitcast.8), custom_call_target="tpu_custom_call" | custom-call | tf_op jit(solution)/shard_map/pallas_call | solution.py:357
  89.8 1.7 %shard_map.84 = (bf16[44,8,2048]{2,1,0:T(8,128)(2,1)}, bf16[44,8,2048]{2,1,0:T(8,128)(2,1)}, f32[8,44]{1,0:T(8,128)}, f32[8,44]{1,0:T(8,128)}, bf16[8,8,2048]{2,1,0:T(8,128)(2,1)}) custom-call(bf16[44,8,2048]{2,1,0:T(8,128)(2,1)S(1)} %get-tuple-element.15.refs_0_, bf16[44,8,2048]{2,1,0:T(8,128)(2,1)S(1)} %get-tuple-element.16.refs_1_, ...), custom_call_target="tpu_custom_call" | custom-call | tf_op jit(solution)/shard_map/pallas_call | solution.py:386

commit v3 on v2

--- a/solution.py
+++ b/solution.py
@@ -303,12 +303,12 @@
 
         return body
 
-    lax.fori_loop(0, N // 2, merge(0, og_ref), 0)
-    lax.fori_loop(0, N // 2, merge(1, ou_ref), 0)
+    def sent(m, i):
+        pltpu.make_async_copy(send.at[m, 0], recv.at[m, 0], send_sem.at[m, i]).wait()
+        return 0
 
     def drain(i, _):
-        bulk(0, i)[1]().wait_send()
-        bulk(1, i)[1]().wait_send()
+        sent(0, i)
         router(i + 1).wait_send()
         has, copy = rs(i + 1)
 
@@ -330,6 +330,10 @@
         return 0
 
     lax.fori_loop(0, GROUPS, x_wait, 0)
+
+    lax.fori_loop(0, N // 2, merge(0, og_ref), 0)
+    lax.fori_loop(0, N - 1, lambda i, _: sent(1, i), 0)
+    lax.fori_loop(0, N // 2, merge(1, ou_ref), 0)
 
 
 def put_out(*refs):

time: 91.7 us -> 90.2 us (0.984)
  Pallas kernels: 90.9 us -> 89.3 us
    pallas_call x1, Pallas kernels: 89.2 us -> 87.6 us  [on_device(): pl.pallas_call(kernel, out_shape=results, in_specs=[hbm] * 4, out_specs=(...]
where the time goes in v3:
time: 90.2 us; the launch traced here: 90 us
  Pallas kernels  89.3 us (99%)
    pallas_call x1, Pallas kernels, on_device(): pl.pallas_call(kernel, out_shape=results, in_specs=[hbm] * 4, out_specs=(...  87.6 us

profile of v3, /device:TPU:1, one launch (start us, length us, event | category | flops | bytes accessed | tf_op | source)
XLA Modules:
  0.0 90.0 jit_solution(17778035823562308480)
XLA Ops:
  0.6 87.6 %shard_map.83 = (bf16[44,8,2048]{2,1,0:T(8,128)(2,1)S(1)}, bf16[44,8,2048]{2,1,0:T(8,128)(2,1)S(1)}, f32[8,44]{1,0:T(8,128)S(1)}, f32[8,44]{1,0:T(8,128)S(1)}, bf16[8,8,2048]{2,1,0:T(8,128)(2,1)S(1)}) custom-call(f32[8,64,1408]{2,1,0:T(8,128)} %wg_ref.1, f32[8,64,1408]{2,1,0:T(8,128)} %wu_ref.1, f32[8,64]{1,0:T(8,128)} %bitcast.7, f32[1,64]{1,0:T(1,128)} %bitcast.8), custom_call_target="tpu_custom_call" | custom-call | tf_op jit(solution)/shard_map/pallas_call | solution.py:361
  88.3 1.7 %shard_map.84 = (bf16[44,8,2048]{2,1,0:T(8,128)(2,1)}, bf16[44,8,2048]{2,1,0:T(8,128)(2,1)}, f32[8,44]{1,0:T(8,128)}, f32[8,44]{1,0:T(8,128)}, bf16[8,8,2048]{2,1,0:T(8,128)(2,1)}) custom-call(bf16[44,8,2048]{2,1,0:T(8,128)(2,1)S(1)} %get-tuple-element.15.refs_0_, bf16[44,8,2048]{2,1,0:T(8,128)(2,1)S(1)} %get-tuple-element.16.refs_1_, ...), custom_call_target="tpu_custom_call" | custom-call | tf_op jit(solution)/shard_map/pallas_call | solution.py:390

commit v4 on v3

--- a/solution.py
+++ b/solution.py
@@ -72,6 +72,9 @@
     mine, owns = tile_of(me)
 
     def offset(i):
+        if isinstance(i, int):
+            g = i // Y
+            return (7 - g) // 2 if g % 2 else 4 + g // 2, (i + 1) % Y
         g = i // Y
         dz = jnp.where(g % 2 == 1, (7 - g) // 2, 4 + g // 2)
         return dz, lax.rem(i + 1, Y)
@@ -164,7 +167,8 @@
 
             return 0
 
-        lax.fori_loop(1, N, body, 0)
+        for k in range(1, N):
+            body(k, 0)
 
     sum_of(0)
     pl.semaphore_wait(barrier, N - 1 + GROUPS - 1)
@@ -180,7 +184,8 @@
             return acc + sums[k]
 
         total[tile(mine)] = lax.fori_loop(1, N, add, part[tile(mine)])
-        lax.fori_loop(1, N, lambda k, _: (ag(k).start(), 0)[1], 0)
+        for k in range(1, N):
+            ag(k).start()
 
     def scale_tile(m, c):
         cols = pl.ds(pl.multiple_of(c * LANES, LANES), LANES)

time: 90.2 us -> 89.8 us (level)
  no operation moved by 1% of the time
where the time goes in v4:
time: 89.8 us; the launch traced here: 89.7 us
  Pallas kernels  89.1 us (99%)
    pallas_call x1, Pallas kernels, on_device(): pl.pallas_call(kernel, out_shape=results, in_specs=[hbm] * 4, out_specs=(...  87.4 us

profile of v4, /device:TPU:1, one launch (start us, length us, event | category | flops | bytes accessed | tf_op | source)
XLA Modules:
  0.0 89.7 jit_solution(16107136351329820768)
XLA Ops:
  0.6 87.4 %shard_map.83 = (bf16[44,8,2048]{2,1,0:T(8,128)(2,1)S(1)}, bf16[44,8,2048]{2,1,0:T(8,128)(2,1)S(1)}, f32[8,44]{1,0:T(8,128)S(1)}, f32[8,44]{1,0:T(8,128)S(1)}, bf16[8,8,2048]{2,1,0:T(8,128)(2,1)S(1)}) custom-call(f32[8,64,1408]{2,1,0:T(8,128)} %wg_ref.1, f32[8,64,1408]{2,1,0:T(8,128)} %wu_ref.1, f32[8,64]{1,0:T(8,128)} %bitcast.7, f32[1,64]{1,0:T(1,128)} %bitcast.8), custom_call_target="tpu_custom_call" | custom-call | tf_op jit(solution)/shard_map/pallas_call | solution.py:366
  88.0 1.7 %shard_map.84 = (bf16[44,8,2048]{2,1,0:T(8,128)(2,1)}, bf16[44,8,2048]{2,1,0:T(8,128)(2,1)}, f32[8,44]{1,0:T(8,128)}, f32[8,44]{1,0:T(8,128)}, bf16[8,8,2048]{2,1,0:T(8,128)(2,1)}) custom-call(bf16[44,8,2048]{2,1,0:T(8,128)(2,1)S(1)} %get-tuple-element.15.refs_0_, bf16[44,8,2048]{2,1,0:T(8,128)(2,1)S(1)} %get-tuple-element.16.refs_1_, ...), custom_call_target="tpu_custom_call" | custom-call | tf_op jit(solution)/shard_map/pallas_call | solution.py:395
